TPU v7x, 32 devices: a whole 2x2x4 slice. The times are simulated.
32 devices in a mesh: pipe: 4 (over y, x), dp: 8 (over z, core).
Axes of the slice: x: 2, y: 2, z: 4, core: 2. Of those that a mesh axis runs over, the one named last changes fastest.
Arguments:
- acts: bfloat16 [4, 2048, 3072], P('pipe', 'dp'), may hold values from -24 to 24, as said below
- grad: float32 [12288, 4096], P('pipe', 'dp'), may hold values from -6 to 6
- owner_of: int32 [4, 12], replicated, may hold values from 0 to 3, as said below
Outputs:
- precond: float32 [12288, 4096], P('pipe', 'dp')
- held_inverse: float32 [4, 24, 256, 256], P('pipe', None, 'dp')
Inputs may be any that keep to these rules, and one draw needn't show every extreme that they name: `acts`: column and token scales of the activations vary; entries lie within the range. `owner_of`: no section index owns more than 24 blocks in all, and some section index owns exactly 24.
All inputs are finite; a program needn't handle non-finite values.
Results may differ from a plain program's by a relative error of at most 0.0003.
Values sent between devices are 32-bit elements; how exact they have to be, the bound alone decides.
A program may use at most 128 MiB of HBM per device.

v0:
```python
import jax
import jax.numpy as jnp
from jax import lax
from jax.sharding import PartitionSpec as P

BLK = 256
HOST = 24
damping_ratio = 0.1


def invert_blocks(factor, vacant):
    order_size = factor.shape[-1]
    diagonal_sum = jnp.sum(jnp.diagonal(factor, axis1=1, axis2=2), axis=1)
    damping = damping_ratio * diagonal_sum / order_size
    identity = jnp.eye(order_size, dtype=factor.dtype)
    shifted = factor + (damping + vacant)[:, None, None] * identity
    cholesky_lower = jnp.linalg.cholesky(shifted)
    identity_stack = jnp.broadcast_to(identity, factor.shape)
    inv_lower = lax.linalg.triangular_solve(
        cholesky_lower, identity_stack, left_side=True, lower=True
    )
    return jnp.einsum("mkr,mkc->mrc", inv_lower, inv_lower, precision=lax.Precision.HIGHEST)


def slot_tables(owner_of):
    owners_flat = owner_of.reshape(-1)
    positions = jnp.arange(owners_flat.shape[0], dtype=jnp.int32)
    matches = owners_flat[:, None] == owners_flat[None, :]
    before = positions[None, :] < positions[:, None]
    slot_rank = jnp.sum((matches & before).astype(jnp.int32), axis=1)
    return (owners_flat, slot_rank)


def shards(acts, grad, owner_of):
    tokens = acts.shape[1]
    feature_count = acts.shape[2]
    nblocks = feature_count // BLK
    data_count = lax.axis_size("dp")
    section_count = lax.axis_size("pipe")
    row_share = BLK // data_count
    all_tokens = tokens * data_count
    section_index = lax.axis_index("pipe")
    member = lax.axis_index("dp")
    features = acts[0].reshape(tokens, nblocks, BLK)
    owners_flat, slot_rank = slot_tables(owner_of)
    slot_ids = jnp.arange(HOST, dtype=jnp.int32)
    pick_mine = (
        (owners_flat[None, :] == section_index) & (slot_rank[None, :] == slot_ids[:, None])
    ).astype(jnp.float32)
    own_owners = lax.dynamic_index_in_dim(owner_of, section_index, 0, keepdims=False)
    own_ranks = lax.dynamic_index_in_dim(
        slot_rank.reshape(section_count, nblocks), section_index, 0, keepdims=False
    )
    target = own_owners * HOST + own_ranks
    pick_back = (
        jnp.arange(section_count * HOST, dtype=jnp.int32)[None, :] == target[:, None]
    ).astype(jnp.float32)
    block_terms = jnp.einsum("tbr,tbc->rbc", features, features, preferred_element_type=jnp.float32)
    my_rows = lax.psum_scatter(
        block_terms.reshape(row_share * lax.axis_size("dp"), nblocks * BLK),
        "dp",
        scatter_dimension=0,
        tiled=True,
    )
    pieces = lax.all_gather(my_rows, "pipe", axis=0, tiled=True).reshape(
        section_count, row_share, nblocks, BLK
    )
    hosted = jnp.einsum(
        "jsb,srbc->jrc",
        pick_mine.reshape(HOST, section_count, nblocks),
        pieces,
        precision=lax.Precision.HIGHEST,
    )
    occupied = jnp.sum(pick_mine, axis=1)
    per_member = (HOST + data_count - 1) // data_count
    padded_count = per_member * data_count
    padded = jnp.pad(hosted, ((0, padded_count - HOST), (0, 0), (0, 0)))
    mine_blocks = lax.all_to_all(padded, "dp", split_axis=0, concat_axis=1, tiled=True) / all_tokens
    padded_flags = jnp.pad(occupied, (0, padded_count - HOST))
    held_flags = lax.dynamic_slice_in_dim(padded_flags, member * per_member, per_member, 0)
    inverted = invert_blocks(mine_blocks, 1.0 - held_flags) * held_flags[:, None, None]
    spread_rows = lax.all_to_all(inverted, "dp", split_axis=1, concat_axis=0, tiled=True)
    held_rows = spread_rows[:HOST]
    returned = lax.all_gather(held_rows, "pipe", axis=0, tiled=True)
    own_rows = jnp.einsum("bm,mrc->brc", pick_back, returned, precision=lax.Precision.HIGHEST)
    inverse = lax.all_gather(own_rows, "dp", axis=1, tiled=True)
    grad_blocks = grad.reshape(nblocks, BLK, grad.shape[1])
    precond = jnp.einsum("brk,bkc->brc", inverse, grad_blocks, precision=lax.Precision.HIGHEST)
    return (precond.reshape(feature_count, grad.shape[1]), held_rows[None])


def solution(mesh):
    placed = (P("pipe", "dp", None), P("pipe", "dp"), P())
    return jax.shard_map(
        shards,
        mesh=mesh,
        in_specs=placed,
        out_specs=(P("pipe", "dp"), P("pipe", None, "dp", None)),
        check_vma=False,
    )
```

profile of v0, /device:TPU:0, one launch (start us, length us, event | category | flops | bytes accessed | tf_op | source)
XLA Modules:
  0.0 447.4 jit_solution(14781126711529102693)
XLA Ops:
  7.2 1.7 copy.123
  8.9 2.3 fusion.30
  11.2 3.5 copy.125
  14.8 43.2 %reduce-scatter.2.cloned.1.call-done = f32[32,3072]{1,0:T(8,128)} async-done(((f32[256,3072]{1,0:T(8,128)}), f32[32,3072]{1,0:T(8,128)}) %reduce-scatter.2.cloned.1.call-update) | async-done | bytes 393232 | tf_op jit(solution)/shard_map/reduce_scatter | solution.py:59
  58.4 31.6 %all-gather.4.cloned.1.call-done = f32[128,3072]{1,0:T(8,128)} async-done(((f32[32,3072]{1,0:T(8,128)}), f32[128,3072]{1,0:T(8,128)}) %all-gather.4.cloned.1.call-update) | async-done | bytes 1572880 | tf_op jit(solution)/shard_map/all_gather | solution.py:65
  90.0 1.7 reshape.95
  91.7 0.9 convolution_bitcast_fusion
  92.6 1.1 copy.127
  93.7 4.6 %all-to-all-start = ((f32[24,32,256]{2,1,0:T(8,128)}), f32[24,32,256]{2,1,0:T(8,128)S(1)}, u32[]{:S(2)}, u32[]{:S(2)}) async-start(f32[24,32,256]{2,1,0:T(8,128)} %copy.127), calls=%async_computation.1 | async-start | bytes 1572864 | tf_op jit(solution)/shard_map/all_to_all | solution.py:78
  98.6 0.7 copy.135
  100.8 0.6 iota_compare_fusion.1
  101.4 17.8 %all-to-all-done = f32[24,32,256]{2,1,0:T(8,128)S(1)} async-done(((f32[24,32,256]{2,1,0:T(8,128)}), f32[24,32,256]{2,1,0:T(8,128)S(1)}, u32[]{:S(2)}, u32[]{:S(2)}) %all-to-all-start) | async-done | bytes 786464 | tf_op jit(solution)/shard_map/all_to_all | solution.py:78
  119.4 16.8 %copy.129 = f32[3,256,256]{0,2,1:T(8,128)} copy(f32[3,256,256]{2,1,0:T(8,128)S(1)} %bitcast.75) | data formatting | bytes 1572864 | tf_op jit(solution)/shard_map/div | solution.py:78
  136.5 2.3 gather_fusion
  140.4 0.8 fusion.5
  141.3 35.2 %custom-call.16 = f32[3,128,128]{2,1,0:T(8,128)S(1)} custom-call(f32[3,128,128]{2,1,0:T(8,128)S(1)} %cholesky.122), custom_call_target="Cholesky" | custom-call | tf_op jit(solution)/shard_map/jit(cholesky)/cholesky | solution.py:17
  176.5 0.8 select_bitcast_fusion
  177.3 29.5 %custom-call.17 = f32[3,1,128,128]{2,3,1,0:T(8,128)S(1)} custom-call(f32[3,1,128,128]{3,2,1,0:T(8,128)S(1)} %select_bitcast_fusion), custom_call_target="InvertDiagBlocksLowerTriangular" | custom-call | tf_op jit(solution)/shard_map/jit(cholesky)/cholesky | solution.py:17
  207.7 35.4 %custom-call.18 = f32[3,128,128]{2,1,0:T(8,128)S(1)} custom-call(f32[3,128,128]{2,1,0:T(8,128)S(1)} %convolution_subtract_fusion.1), custom_call_target="Cholesky" | custom-call | tf_op jit(solution)/shard_map/jit(cholesky)/cholesky | solution.py:17
  243.6 5.4 %while.1 = (s32[]{:T(128)}, f32[3,256,256]{2,1,0:T(8,128)S(1)}, s32[2,2]{1,0:T(2,128)S(1)}, f32[2,3,128,128]{3,2,0,1:T(8,128)}, s32[]{:T(128)}) while((s32[]{:T(128)}, f32[3,256,256]{2,1,0:T(8,128)S(1)}, s32[2,2]{1,0:T(2,128)S(1)}, f32[2,3,128,128]{3,2,0,1:T(8,128)}, s32[]{:T(128)}) %tuple.29), condition=%wide.while_cond, body=%wide.while_body.sunk | while | flops 2 | bytes 394849 | solution.py:19
  244.2 2.1 bitcast_dynamic-update-slice_fusion.2
  246.9 2.1 bitcast_dynamic-update-slice_fusion.2
  248.9 59.8 %custom-call.19 = f32[3,2,128,128]{2,3,1,0:T(8,128)S(1)} custom-call(f32[3,2,128,128]{3,2,1,0:T(8,128)} %bitcast.83), custom_call_target="InvertDiagBlocksLowerTriangular" | custom-call | tf_op jit(solution)/shard_map/triangular_solve | solution.py:19
  310.3 1.4 convolution_multiply_fusion
  312.3 29.0 %all_to_all.27 = f32[3,256,256]{2,0,1:T(4,128)S(1)} all-to-all(f32[3,256,256]{2,0,1:T(4,128)S(1)} %copy.140), channel_id=1, replica_groups=mesh['pipe'=4,'dp'=8] {'dp'}, dimensions={1} | all-to-all | bytes 1572864 | tf_op jit(solution)/shard_map/all_to_all | solution.py:82
  341.4 1.0 copy.142
  342.7 0.7 fusion.26
  343.4 40.9 %all-gather.6.cloned.1.call-done = f32[96,32,256]{2,1,0:T(8,128)} async-done(((f32[24,32,256]{2,1,0:T(8,128)}), f32[96,32,256]{2,1,0:T(8,128)}) %all-gather.6.cloned.1.call-update) | async-done | bytes 3145744 | tf_op jit(solution)/shard_map/all_gather | solution.py:84
  384.4 4.7 %fusion = f32[12,32,256]{2,0,1:T(8,128)S(1)} fusion(f32[96,32,256]{2,1,0:T(8,128)} %all-gather.6.cloned.1.call-done, s32[12]{0:T(128)S(1)} %fusion.26), kind=kOutput, calls=%fused_computation.3 | convolution fusion | flops 113247360 | bytes 3538992 | tf_op jit(solution)/shard_map/bm,mrc->brc/dot_general | solution.py:85
  389.0 1.0 copy.144
  390.0 38.4 %all-gather.8.cloned.1.call-done = f32[12,256,256]{2,1,0:T(8,128)} async-done(((f32[12,32,256]{2,1,0:T(8,128)}), f32[12,256,256]{2,1,0:T(8,128)}) %all-gather.8.cloned.1.call-update) | async-done | bytes 3145744 | tf_op jit(solution)/shard_map/all_gather | solution.py:86
  428.4 12.5 %fusion.31 = f32[12,256,512]{2,1,0:T(8,128)} fusion(f32[12,256,256]{2,1,0:T(8,128)} %all-gather.8.cloned.1.call-done, f32[12,256,512]{2,1,0:T(8,128)} %bitcast.77), kind=kOutput, calls=%fused_computation.66 | convolution fusion | flops 4831838208 | bytes 15728640 | tf_op jit(solution)/shard_map/brk,bkc->brc/dot_general | solution.py:88
  (61 shorter events, 9.3 us)
Async XLA Ops:
  7.2 50.8 %reduce-scatter.2.cloned.1.call-start = ((), (), s32[]{:S(2)}) async-start(), calls=%async_computation.3 | async-start | bytes 3538944 | tf_op jit(solution)/shard_map/reduce_scatter | solution.py:59
  14.7 43.3 %copy-start.2 = (s32[4,12]{1,0:T(4,128)S(1)}, s32[4,12]{1,0:T(4,128)}, u32[]{:S(2)}) copy-start(s32[4,12]{1,0:T(4,128)} %param.5) | copy-start | bytes 580
  14.7 75.2 %all-gather.4.cloned.1.call-start = ((), (), s32[]{:S(2)}) async-start(), calls=%async_computation.4 | async-start | bytes 1966080 | tf_op jit(solution)/shard_map/all_gather | solution.py:65
  58.4 34.2 %copy-start.3 = (s32[4,12]{1,0:T(4,128)}, s32[4,12]{1,0:T(4,128)S(1)}, u32[]{:S(2)}) copy-start(s32[4,12]{1,0:T(4,128)S(1)} %reshape.93) | copy-start | bytes 580
  93.7 25.6 %all-to-all-start = ((f32[24,32,256]{2,1,0:T(8,128)}), f32[24,32,256]{2,1,0:T(8,128)S(1)}, u32[]{:S(2)}, u32[]{:S(2)}) async-start(f32[24,32,256]{2,1,0:T(8,128)} %copy.127), calls=%async_computation.1 | async-start | bytes 1572864 | tf_op jit(solution)/shard_map/all_to_all | solution.py:78
  98.3 286.0 %all-gather.6.cloned.1.call-start = ((), (), s32[]{:S(2)}) async-start(), calls=%async_computation.5 | async-start | bytes 3932160 | tf_op jit(solution)/shard_map/all_gather | solution.py:84
  139.4 0.5 copy-start.4
  140.4 102.9 %copy-start.1 = (pred[256,256]{1,0:T(8,128)(4,1)S(1)}, pred[256,256]{1,0:T(8,128)(4,1)}, u32[]{:S(2)}) copy-start(pred[256,256]{1,0:T(8,128)(4,1)} %iota_compare_fusion.1) | copy-start | bytes 196612
  141.2 102.3 %copy-start.6 = (s32[2]{0:T(128)S(1)}, s32[2]{0:T(128)}, u32[]{:S(2)}) copy-start(s32[2]{0:T(128)} %iota_multiply_fusion) | copy-start | bytes 28
  176.5 132.2 %copy-start = (f32[128,256]{1,0:T(8,128)S(1)}, f32[128,256]{1,0:T(8,128)}, u32[]{:S(2)}) copy-start(f32[128,256]{1,0:T(8,128)} %copy.135) | copy-start | bytes 393220
  243.3 67.0 %copy-start.5 = (f32[3]{0:T(128)S(1)}, f32[3]{0:T(128)}, u32[]{:S(2)}) copy-start(f32[3]{0:T(128)} %get-tuple-element.21) | copy-start | bytes 40
  342.4 86.0 %all-gather.8.cloned.1.call-start = ((), (), s32[]{:S(2)}) async-start(), calls=%async_computation.6 | async-start | bytes 3538944 | tf_op jit(solution)/shard_map/all_gather | solution.py:86
Sparse Core Ops, SparseCore 0:
  14.9 43.0 reduce-scatter.1
  59.8 30.0 all-gather.3
  342.5 41.7 all-gather.5
  390.1 38.1 all-gather.7
where the time goes:
time: 448 us; the launch traced here: 447 us
  waiting for transfers between devices  172 us (38%)
  other arithmetic  165 us (37%)
  local copies, waits for them, and re-layouts  37.5 us (8%)
  blocking collectives  29 us (6%)
  matrix products  24.2 us (5%)
  between operations  14.1 us (3%)
  starting transfers between devices  5.21 us (1%)
    another operation x9, other arithmetic, invert_blocks(): cholesky_lower = jnp.linalg.cholesky(shifted)  102 us
    another operation x4, other arithmetic, invert_blocks(): lax.linalg.triangular_solve(cholesky_lower, identity_stack, left_side=Tru...  61.1 us
    reduce_scatter x1, waiting for transfers between devices, shards(): lax.psum_scatter(block_terms.reshape(row_share * lax.axis_size('dp'), nbl...  43.2 us
    all_gather x1, waiting for transfers between devices, shards(): returned = lax.all_gather(held_rows, 'pipe', axis=0, tiled=True)  40.9 us
    all_gather x1, waiting for transfers between devices, shards(): inverse = lax.all_gather(own_rows, 'dp', axis=1, tiled=True)  38.4 us
    all_gather x1, waiting for transfers between devices, shards(): lax.all_gather(my_rows, 'pipe', axis=0, tiled=True)  31.6 us
    all_to_all x1, blocking collectives, shards(): lax.all_to_all(inverted, 'dp', split_axis=1, concat_axis=0, tiled=True)  29 us
    all_to_all x1, waiting for transfers between devices, shards(): lax.all_to_all(padded, 'dp', split_axis=0, concat_axis=1, tiled=True)  17.8 us
  transfers between devices with their start and end apart: 5, of which 5 were waited for; matrix products, arithmetic and copies ran while one was open for 1% of the time, Pallas kernels for 0%

commit v1 on v0

--- a/solution.py
+++ b/solution.py
@@ -32,6 +32,43 @@
 
 
 def shards(acts, grad, owner_of):
+
+    def track_patches_by_axis(local_values, packet):
+        chip_axis = "dp"
+        base_arr, piece_out, x_now = (
+            lax.axis_size(chip_axis),
+            lax.axis_index(chip_axis),
+            local_values.shape[1],
+        )
+        so_far_all = tuple(((src_i, (src_i + 1) % base_arr) for src_i in range(base_arr)))
+        pieces_in = tuple(((j, i) for i, j in so_far_all))
+        x_new, z2 = (
+            lax.ppermute(local_values, axis_name=chip_axis, perm=so_far_all),
+            lax.ppermute(local_values, axis_name=chip_axis, perm=pieces_in),
+        )
+        seen_now = packet(local_values, piece_out * x_now)
+        met_up = seen_now.shape[1]
+        answer = jnp.zeros(
+            (*seen_now.shape[:1], base_arr * met_up, *seen_now.shape[2:]), seen_now.dtype
+        )
+
+        def _draw_sheets(answer, seen_now, z):
+            return lax.dynamic_update_slice_in_dim(answer, seen_now, z * met_up, axis=1)
+
+        answer = _draw_sheets(answer, seen_now, piece_out)
+        for idx in [*range(1, base_arr // 2 + 1)]:
+            e_next, v_next = ((piece_out - idx) % base_arr, (piece_out + idx) % base_arr)
+            w1 = (x_new, z2)
+            if idx < base_arr // 2:
+                x_new, z2 = (
+                    lax.ppermute(x_new, axis_name=chip_axis, perm=so_far_all),
+                    lax.ppermute(z2, axis_name=chip_axis, perm=pieces_in),
+                )
+            answer = _draw_sheets(answer, packet(w1[0], e_next * x_now), e_next)
+            if 2 * idx < base_arr:
+                answer = _draw_sheets(answer, packet(w1[1], v_next * x_now), v_next)
+        return answer
+
     tokens = acts.shape[1]
     feature_count = acts.shape[2]
     nblocks = feature_count // BLK
@@ -83,9 +120,13 @@
     held_rows = spread_rows[:HOST]
     returned = lax.all_gather(held_rows, "pipe", axis=0, tiled=True)
     own_rows = jnp.einsum("bm,mrc->brc", pick_back, returned, precision=lax.Precision.HIGHEST)
-    inverse = lax.all_gather(own_rows, "dp", axis=1, tiled=True)
     grad_blocks = grad.reshape(nblocks, BLK, grad.shape[1])
-    precond = jnp.einsum("brk,bkc->brc", inverse, grad_blocks, precision=lax.Precision.HIGHEST)
+    precond = track_patches_by_axis(
+        own_rows,
+        packet=lambda part, offset: jnp.einsum(
+            "brk,bkc->brc", part, grad_blocks, precision=lax.Precision.HIGHEST
+        ),
+    )
     return (precond.reshape(feature_count, grad.shape[1]), held_rows[None])
 
 

time: 448 us -> 462 us (1.031)
  waiting for transfers between devices: 172 us -> 149 us
  matrix products: 24.2 us -> 42.3 us
  starting transfers between devices: 5.21 us -> 16.7 us
    all_gather x1 -> x0, waiting for transfers between devices: 38.4 us -> none  [shards(): inverse = lax.all_gather(own_rows, 'dp', axis=1, tiled=True)]
    dot_general x1 -> x8, matrix products: 12.5 us -> 32.1 us  [shards(): jnp.einsum('brk,bkc->brc', part, grad_blocks, precision=lax.Precision.HIG...]
    ppermute x0 -> x7, waiting for transfers between devices: none -> 15.3 us  [the longest x3 11.3 us: track_patches_by_axis(): lax.ppermute(x_new, axis_name=chip_axis, perm=so_far_all)]
    ppermute x0 -> x7, starting transfers between devices: none -> 11.4 us  [the longest x2 7.47 us: track_patches_by_axis(): lax.ppermute(z2, axis_name=chip_axis, perm=pieces_in)]
  transfers between devices with their start and end apart: 5 -> 11, of which waited for: 5 -> 8; matrix products, arithmetic and copies ran while one was open for 1% -> 7% of each run, Pallas kernels for 0% -> 0%
where the time goes in v1:
time: 462 us; the launch traced here: 458 us
  other arithmetic  166 us (36%)
  waiting for transfers between devices  149 us (32%)
  matrix products  42.3 us (9%)
  local copies, waits for them, and re-layouts  40.8 us (9%)
  blocking collectives  29 us (6%)
  starting transfers between devices  16.7 us (4%)
  between operations  14.5 us (3%)
    another operation x9, other arithmetic, invert_blocks(): cholesky_lower = jnp.linalg.cholesky(shifted)  102 us
    another operation x4, other arithmetic, invert_blocks(): lax.linalg.triangular_solve(cholesky_lower, identity_stack, left_side=Tru...  62 us
    reduce_scatter x1, waiting for transfers between devices, shards(): lax.psum_scatter(block_terms.reshape(row_share * lax.axis_size('dp'), nbl...  43.2 us
    all_gather x1, waiting for transfers between devices, shards(): returned = lax.all_gather(held_rows, 'pipe', axis=0, tiled=True)  41.1 us
    dot_general x8, matrix products, shards(): jnp.einsum('brk,bkc->brc', part, grad_blocks, precision=lax.Precision.HIG...  32.1 us
    all_gather x1, waiting for transfers between devices, shards(): lax.all_gather(my_rows, 'pipe', axis=0, tiled=True)  31.6 us
    all_to_all x1, blocking collectives, shards(): lax.all_to_all(inverted, 'dp', split_axis=1, concat_axis=0, tiled=True)  29 us
    all_to_all x1, waiting for transfers between devices, shards(): lax.all_to_all(padded, 'dp', split_axis=0, concat_axis=1, tiled=True)  17.5 us
  transfers between devices with their start and end apart: 11, of which 8 were waited for; matrix products, arithmetic and copies ran while one was open for 7% of the time, Pallas kernels for 0%

profile of v1, /device:TPU:0, one launch (start us, length us, event | category | flops | bytes accessed | tf_op | source)
XLA Modules:
  0.0 458.4 jit_solution(13112569910328553083)
XLA Ops:
  8.9 2.3 fusion.37
  11.2 3.5 copy.141
  14.8 43.2 %reduce-scatter.2.cloned.1.call-done = f32[32,3072]{1,0:T(8,128)} async-done(((f32[256,3072]{1,0:T(8,128)}), f32[32,3072]{1,0:T(8,128)}) %reduce-scatter.2.cloned.1.call-update) | async-done | bytes 393232 | tf_op jit(solution)/shard_map/reduce_scatter | solution.py:96
  58.4 31.6 %all-gather.3.cloned.1.call-done = f32[128,3072]{1,0:T(8,128)} async-done(((f32[32,3072]{1,0:T(8,128)}), f32[128,3072]{1,0:T(8,128)}) %all-gather.3.cloned.1.call-update) | async-done | bytes 1572880 | tf_op jit(solution)/shard_map/all_gather | solution.py:102
  93.8 4.6 %all-to-all-start = ((f32[24,32,256]{2,1,0:T(8,128)}), f32[24,32,256]{2,1,0:T(8,128)S(1)}, u32[]{:S(2)}, u32[]{:S(2)}) async-start(f32[24,32,256]{2,1,0:T(8,128)} %copy.143), calls=%async_computation.1 | async-start | bytes 1572864 | tf_op jit(solution)/shard_map/all_to_all | solution.py:115
  101.8 17.5 %all-to-all-done = f32[24,32,256]{2,1,0:T(8,128)S(1)} async-done(((f32[24,32,256]{2,1,0:T(8,128)}), f32[24,32,256]{2,1,0:T(8,128)S(1)}, u32[]{:S(2)}, u32[]{:S(2)}) %all-to-all-start) | async-done | bytes 786464 | tf_op jit(solution)/shard_map/all_to_all | solution.py:115
  119.5 16.8 %copy.145 = f32[3,256,256]{0,2,1:T(8,128)} copy(f32[3,256,256]{2,1,0:T(8,128)S(1)} %bitcast.92) | data formatting | bytes 1572864 | tf_op jit(solution)/shard_map/div | solution.py:115
  136.5 2.3 gather_fusion
  141.3 35.2 %custom-call.16 = f32[3,128,128]{2,1,0:T(8,128)S(1)} custom-call(f32[3,128,128]{2,1,0:T(8,128)S(1)} %cholesky.122), custom_call_target="Cholesky" | custom-call | tf_op jit(solution)/shard_map/jit(cholesky)/cholesky | solution.py:17
  177.3 29.5 %custom-call.17 = f32[3,1,128,128]{2,3,1,0:T(8,128)S(1)} custom-call(f32[3,1,128,128]{3,2,1,0:T(8,128)S(1)} %select_bitcast_fusion), custom_call_target="InvertDiagBlocksLowerTriangular" | custom-call | tf_op jit(solution)/shard_map/jit(cholesky)/cholesky | solution.py:17
  207.7 35.3 %custom-call.18 = f32[3,128,128]{2,1,0:T(8,128)S(1)} custom-call(f32[3,128,128]{2,1,0:T(8,128)S(1)} %convolution_subtract_fusion.1), custom_call_target="Cholesky" | custom-call | tf_op jit(solution)/shard_map/jit(cholesky)/cholesky | solution.py:17
  245.0 5.1 %while.1 = (s32[]{:T(128)}, f32[3,256,256]{2,1,0:T(8,128)S(1)}, s32[2,2]{1,0:T(2,128)S(1)}, f32[2,3,128,128]{3,2,0,1:T(8,128)}, s32[]{:T(128)}) while((s32[]{:T(128)}, f32[3,256,256]{2,1,0:T(8,128)S(1)}, s32[2,2]{1,0:T(2,128)S(1)}, f32[2,3,128,128]{3,2,0,1:T(8,128)}, s32[]{:T(128)}) %tuple.29), condition=%wide.while_cond, body=%wide.while_body.sunk | while | flops 2 | bytes 394849 | solution.py:19
  250.1 59.8 %custom-call.19 = f32[3,2,128,128]{2,3,1,0:T(8,128)S(1)} custom-call(f32[3,2,128,128]{3,2,1,0:T(8,128)} %bitcast.99), custom_call_target="InvertDiagBlocksLowerTriangular" | custom-call | tf_op jit(solution)/shard_map/triangular_solve | solution.py:19
  313.4 29.0 %all_to_all.27 = f32[3,256,256]{2,0,1:T(4,128)S(1)} all-to-all(f32[3,256,256]{2,0,1:T(4,128)S(1)} %copy.156), channel_id=1, replica_groups=mesh['pipe'=4,'dp'=8] {'dp'}, dimensions={1} | all-to-all | bytes 1572864 | tf_op jit(solution)/shard_map/all_to_all | solution.py:119
  344.9 41.1 %all-gather.5.cloned.1.call-done = f32[96,32,256]{2,0,1:T(8,128)} async-done(((f32[24,32,256]{2,0,1:T(8,128)}), f32[96,32,256]{2,0,1:T(8,128)}) %all-gather.5.cloned.1.call-update) | async-done | bytes 3145744 | tf_op jit(solution)/shard_map/all_gather | solution.py:121
  386.0 3.2 fusion.28
  389.4 3.5 collective-permute-start.1
  393.7 5.8 %convolution_dynamic-update-slice_fusion.7 = f32[12,256,512]{2,1,0:T(8,128)S(1)} fusion(f32[12,256,512]{2,1,0:T(8,128)S(1)} %broadcast_in_dim.14, s32[]{:T(128)S(6)} %select_n.74, f32[12,256,512]{2,1,0:T(8,128)} %bitcast.79, f32[12,32,256]{2,0,1:T(8,128)S(1)} %fusion.28), kind=kOutput, calls=%fused_computation.10 | convolution fusion | flops 603979776 | bytes 7602180 | tf_op jit(solution)/shard_map/brk,bkc->brc/dot_general | solution.py:126
  399.6 4.0 collective-permute-done
  403.6 3.5 collective-permute-start.3
  407.2 3.8 convolution_dynamic-update-slice_fusion.6
  410.9 3.8 convolution_dynamic-update-slice_fusion.5
  414.7 4.9 %collective-permute-done.2 = f32[12,32,256]{2,0,1:T(8,128)S(1)} collective-permute-done((f32[12,32,256]{2,0,1:T(8,128)S(1)}, f32[12,32,256]{2,0,1:T(8,128)S(1)}, u32[]{:S(2)}, u32[]{:S(2)}) %collective-permute-start.2) | collective-permute-done | bytes 393248 | tf_op jit(solution)/shard_map/ppermute | solution.py:64
  419.6 3.9 collective-permute-start.5
  423.5 3.8 convolution_dynamic-update-slice_fusion.4
  427.3 3.8 convolution_dynamic-update-slice_fusion.3
  431.1 3.6 collective-permute-done.4
  434.8 3.8 convolution_dynamic-update-slice_fusion.2
  438.6 3.8 convolution_dynamic-update-slice_fusion.1
  442.3 2.8 collective-permute-done.6
  445.2 3.8 convolution_dynamic-update-slice_fusion
  449.0 2.7 copy-done
  (85 shorter events, 27.9 us)
Async XLA Ops:
  7.2 50.8 %reduce-scatter.2.cloned.1.call-start = ((), (), s32[]{:S(2)}) async-start(), calls=%async_computation.3 | async-start | bytes 3538944 | tf_op jit(solution)/shard_map/reduce_scatter | solution.py:96
  11.2 46.8 %copy-start.3 = (s32[4,12]{1,0:T(4,128)S(1)}, s32[4,12]{1,0:T(4,128)}, u32[]{:S(2)}) copy-start(s32[4,12]{1,0:T(4,128)} %param.5) | copy-start | bytes 580
  14.8 75.3 %all-gather.3.cloned.1.call-start = ((), (), s32[]{:S(2)}) async-start(), calls=%async_computation.4 | async-start | bytes 1966080 | tf_op jit(solution)/shard_map/all_gather | solution.py:102
  58.4 61.0 %copy-start.4 = (s32[4,12]{1,0:T(4,128)}, s32[4,12]{1,0:T(4,128)S(1)}, u32[]{:S(2)}) copy-start(s32[4,12]{1,0:T(4,128)S(1)} %reshape.93) | copy-start | bytes 580
  93.8 25.6 %all-to-all-start = ((f32[24,32,256]{2,1,0:T(8,128)}), f32[24,32,256]{2,1,0:T(8,128)S(1)}, u32[]{:S(2)}, u32[]{:S(2)}) async-start(f32[24,32,256]{2,1,0:T(8,128)} %copy.143), calls=%async_computation.1 | async-start | bytes 1572864 | tf_op jit(solution)/shard_map/all_to_all | solution.py:115
  98.4 287.6 %all-gather.5.cloned.1.call-start = ((), (), s32[]{:S(2)}) async-start(), calls=%async_computation.5 | async-start | bytes 3932160 | tf_op jit(solution)/shard_map/all_gather | solution.py:121
  139.5 0.5 copy-start.5
  140.4 169.4 %copy-start.2 = (f32[128,256]{1,0:T(8,128)S(1)}, f32[128,256]{1,0:T(8,128)}, u32[]{:S(2)}) copy-start(f32[128,256]{1,0:T(8,128)} %copy.151) | copy-start | bytes 393220
  141.3 170.2 %copy-start.6 = (f32[3]{0:T(128)S(1)}, f32[3]{0:T(128)}, u32[]{:S(2)}) copy-start(f32[3]{0:T(128)} %get-tuple-element.21) | copy-start | bytes 40
  342.6 56.9 %copy-start.1 = (f32[8,3,32,256]{3,2,1,0:T(8,128)}, f32[8,3,32,256]{3,2,1,0:T(8,128)S(1)}, u32[]{:S(2)}) copy-start(f32[8,3,32,256]{3,2,1,0:T(8,128)S(1)} %copy.158) | copy-start | bytes 2359300
  386.0 21.2 %slice-start = ((s8[6291456]{0:T(1024)(128)(4,1)}), s8[4194304]{0:T(1024)(128)(4,1)S(1)}, s32[]{:S(2)}) async-start(s8[6291456]{0:T(1024)(128)(4,1)} %bitcast.80), calls=%async_computation.6 | async-start | bytes 8388608
  389.1 14.5 %collective-permute-start = (f32[12,32,256]{2,0,1:T(8,128)S(1)}, f32[12,32,256]{2,0,1:T(8,128)S(1)}, u32[]{:S(2)}, u32[]{:S(2)}) collective-permute-start(f32[12,32,256]{2,0,1:T(8,128)S(1)} %fusion.28), channel_id=1, source_target_pairs={{0,1},{1,2},{2,3},{3,4},{4,5},{5,6},{6,7},{7,0},{8,9},{9,10},{10,1... | collective-permute-start | bytes 1179656 | tf_op jit(solution)/shard_map/ppermute | solution.py:46
  389.4 14.2 %collective-permute-start.1 = (f32[12,32,256]{2,0,1:T(8,128)S(1)}, f32[12,32,256]{2,0,1:T(8,128)S(1)}, u32[]{:S(2)}, u32[]{:S(2)}) collective-permute-start(f32[12,32,256]{2,0,1:T(8,128)S(1)} %fusion.28), channel_id=1, source_target_pairs={{1,0},{2,1},{3,2},{4,3},{5,4},{6,5},{7,6},{0,7},{9,8},{10,9},{11,1... | collective-permute-start | bytes 1179656 | tf_op jit(solution)/shard_map/ppermute | solution.py:47
  392.9 14.2 %slice-start.1 = ((s8[6291456]{0:T(1024)(128)(4,1)}), s8[2097152]{0:T(1024)(128)(4,1)S(1)}, s32[]{:S(2)}) async-start(s8[6291456]{0:T(1024)(128)(4,1)} %bitcast.80), calls=%async_computation.7 | async-start | bytes 4194304
  403.6 16.0 %collective-permute-start.2 = (f32[12,32,256]{2,0,1:T(8,128)S(1)}, f32[12,32,256]{2,0,1:T(8,128)S(1)}, u32[]{:S(2)}, u32[]{:S(2)}) collective-permute-start(f32[12,32,256]{2,0,1:T(8,128)S(1)} %collective-permute-done), channel_id=1, source_target_pairs={{0,1},{1,2},{2,3},{3,4},{4,5},{5,6},{6,7},{7,0},{8,9},{9,10},{10,1... | collective-permute-start | bytes 1179656 | tf_op jit(solution)/shard_map/ppermute | solution.py:64
  403.6 16.0 %collective-permute-start.3 = (f32[12,32,256]{2,0,1:T(8,128)S(1)}, f32[12,32,256]{2,0,1:T(8,128)S(1)}, u32[]{:S(2)}, u32[]{:S(2)}) collective-permute-start(f32[12,32,256]{2,0,1:T(8,128)S(1)} %collective-permute-done.1), channel_id=1, source_target_pairs={{1,0},{2,1},{3,2},{4,3},{5,4},{6,5},{7,6},{0,7},{9,8},{10,9},{11,1... | collective-permute-start | bytes 1179656 | tf_op jit(solution)/shard_map/ppermute | solution.py:65
  419.6 15.0 %collective-permute-start.4 = (f32[12,32,256]{2,0,1:T(8,128)S(1)}, f32[12,32,256]{2,0,1:T(8,128)S(1)}, u32[]{:S(2)}, u32[]{:S(2)}) collective-permute-start(f32[12,32,256]{2,0,1:T(8,128)S(1)} %collective-permute-done.2), channel_id=1, source_target_pairs={{0,1},{1,2},{2,3},{3,4},{4,5},{5,6},{6,7},{7,0},{8,9},{9,10},{10,1... | collective-permute-start | bytes 1179656 | tf_op jit(solution)/shard_map/ppermute | solution.py:64
  419.6 19.0 %collective-permute-start.5 = (f32[12,32,256]{2,0,1:T(8,128)S(1)}, f32[12,32,256]{2,0,1:T(8,128)S(1)}, u32[]{:S(2)}, u32[]{:S(2)}) collective-permute-start(f32[12,32,256]{2,0,1:T(8,128)S(1)} %collective-permute-done.3), channel_id=1, source_target_pairs={{1,0},{2,1},{3,2},{4,3},{5,4},{6,5},{7,6},{0,7},{9,8},{10,9},{11,1... | collective-permute-start | bytes 1179656 | tf_op jit(solution)/shard_map/ppermute | solution.py:65
  434.6 10.6 %collective-permute-start.6 = (f32[12,32,256]{2,0,1:T(8,128)S(1)}, f32[12,32,256]{2,0,1:T(8,128)S(1)}, u32[]{:S(2)}, u32[]{:S(2)}) collective-permute-start(f32[12,32,256]{2,0,1:T(8,128)S(1)} %collective-permute-done.4), channel_id=1, source_target_pairs={{0,1},{1,2},{2,3},{3,4},{4,5},{5,6},{6,7},{7,0},{8,9},{9,10},{10,1... | collective-permute-start | bytes 1179656 | tf_op jit(solution)/shard_map/ppermute | solution.py:64
  449.0 2.7 copy-start
Sparse Core Ops, SparseCore 0:
  14.9 43.0 reduce-scatter.1
  59.8 30.1 all-gather.2
  344.1 41.7 all-gather.4
